TPU v7x, 256 devices: a whole 4x4x8 slice. The times are simulated.
256 devices in a mesh: atom: 32 (over y_lo, z, core), band: 8 (over y_hi, x).
Axes of the slice: x: 4, y: 4 (y_hi: 2, y_lo: 2; y = y_hi * 2 + y_lo), z: 8, core: 2. Of those that a mesh axis runs over, the one named last changes fastest.
Arguments:
- wave_rows: bfloat16 [512, 65536], P('atom', 'band'), may hold values from -6 to 6
- projectors: bfloat16 [4096, 65536], P('atom', 'band'), may hold values from -0.0234375 to 0.0234375
- dij_table: float32 [16, 8, 8], replicated, may hold values from -6 to 6
- dij_index: int32 [512], P('atom'), may hold values from 0 to 15
- proj_count: int32 [512], P('atom'), may hold values from 1 to 8
Outputs:
- nonlocal_rows: bfloat16 [512, 65536], P('atom', 'band')
All inputs are finite; a program needn't handle non-finite values.
Results may differ from a plain program's by a relative error of at most 0.0049.
Values may be sent and summed in bfloat16 or wider, within the bound.
A program may use at most 128 MiB of HBM per device.

v0:
```python
import jax
import jax.numpy as jnp
from jax import lax
from jax.sharding import Mesh
from jax.sharding import PartitionSpec as P

ATOM = ("atom_0", "atom_1", "atom_2")


def cut_along(shard, dim, count):
    before, after = (shard.shape[:dim], shard.shape[dim + 1 :])
    return jnp.moveaxis(shard.reshape(*before, count, -1, *after), dim, 0)


def sum_at_owner(shard, axis, dim):
    count = lax.axis_size(axis)
    blocks = lax.all_to_all(cut_along(shard, dim, count), axis, 0, 0, tiled=True)
    return jnp.sum(blocks, axis=0)


def sent_to_all(shard, axis):
    count = lax.axis_size(axis)
    return lax.all_to_all(
        jnp.broadcast_to(shard[None], (count, *shard.shape)), axis, 0, 0, tiled=True
    )


def in_order(blocks, dim):
    blocks = jnp.moveaxis(blocks, 0, dim)
    lengths = blocks.shape
    return blocks.reshape(*lengths[:dim], lengths[dim] * lengths[dim + 1], *lengths[dim + 2 :])


def gathered_copies(shard, axis, dim):
    blocks = sent_to_all(shard, axis)
    return in_order(blocks, dim)


def scatter_pairs(shard, chips, core, dim):
    sizes = (lax.axis_size(chips), lax.axis_size(core))
    blocks = cut_along(shard, dim, sizes[0] * sizes[1])
    inside = blocks.shape[1:]
    blocks = blocks.reshape(*sizes, *inside).swapaxes(0, 1).reshape(-1, *inside)
    blocks = lax.psum_scatter(blocks, core, scatter_dimension=0, tiled=True)
    return lax.psum_scatter(blocks, chips, scatter_dimension=0, tiled=True)[0]


def shards(wave_rows, projectors, dij_table, dij_index, proj_count):
    atom_local = dij_index.shape[0]
    kind_total = dij_table.shape[0]
    per_atom = dij_table.shape[1]
    width = atom_local * per_atom
    partial_value = lax.dot_general(
        lax.all_gather(wave_rows, ATOM, axis=0, tiled=True),
        projectors,
        (((1,), (1,)), ((), ())),
        preferred_element_type=jnp.float32,
    )
    kind_onehot = (dij_index[:, None] == jnp.arange(kind_total, dtype=jnp.int32)[None, :]).astype(
        jnp.float32
    )
    blocks = jnp.dot(
        kind_onehot,
        dij_table.reshape(kind_total, per_atom * per_atom),
        precision=lax.Precision.HIGHEST,
    ).reshape(atom_local, per_atom, per_atom)
    active = (jnp.arange(per_atom, dtype=jnp.int32)[None, :] < proj_count[:, None]).astype(
        jnp.float32
    )
    blocks = blocks * active[:, :, None] * active[:, None, :]
    share = sum_at_owner(partial_value, "band", 0)
    count = share.shape[0]
    mixed = jnp.einsum(
        "baj,aij->bai",
        share.reshape(count, atom_local, per_atom),
        blocks,
        precision=lax.Precision.HIGHEST,
    )
    weighted = gathered_copies(mixed.reshape(count, width).astype(jnp.bfloat16), "band", 0)
    result = scatter_pairs(
        jnp.dot(weighted, projectors, preferred_element_type=jnp.float32),
        ("atom_0", "atom_1"),
        "atom_2",
        0,
    )
    return result.astype(jnp.bfloat16)


def solution(mesh):
    split = Mesh(
        mesh.devices.reshape(2, 8, 2, mesh.shape["band"]), ("atom_0", "atom_1", "atom_2", "band")
    )
    return jax.shard_map(
        shards,
        mesh=split,
        in_specs=(P(ATOM, "band"), P(ATOM, "band"), P(), P(ATOM), P(ATOM)),
        out_specs=P(ATOM, "band"),
        check_vma=False,
    )
```

profile of v0, /device:TPU:1, one launch (start us, length us, event | category | flops | bytes accessed | tf_op | source)
XLA Modules:
  0.0 265.8 jit_solution(16585991134371336601)
XLA Ops:
  6.5 0.0 copy-start
  6.5 0.0 all-gather.2.cloned.1.call-start
  6.6 0.7 all-gather.2.cloned.1.call-update
  7.3 77.8 %all-gather.2.cloned.1.call-done = bf16[512,8192]{1,0:T(8,128)(2,1)} async-done(((bf16[16,8192]{1,0:T(8,128)(2,1)}), bf16[512,8192]{1,0:T(8,128)(2,1)}) %all-gather.2.cloned.1.call-update) | async-done | bytes 8388624 | tf_op jit(solution)/shard_map/all_gather | solution.py:54
  85.1 0.0 copy-done
  85.1 6.4 %fusion.9 = f32[512,128]{1,0:T(8,128)} fusion(bf16[512,8192]{1,0:T(8,128)(2,1)} %all-gather.2.cloned.1.call-done, bf16[128,8192]{1,0:T(8,128)(2,1)S(1)} %copy-done), kind=kOutput, calls=%fused_computation.14 | convolution fusion | flops 1073741824 | bytes 10747904 | tf_op jit(solution)/shard_map/dot_general | solution.py:53
  91.5 6.5 %all-to-all-start = ((f32[8,64,128]{2,1,0:T(8,128)}), f32[8,64,128]{2,1,0:T(8,128)S(1)}, u32[]{:S(2)}, u32[]{:S(2)}) async-start(f32[8,64,128]{2,1,0:T(8,128)} %bitcast.4), calls=%async_computation | async-start | bytes 524288 | tf_op jit(solution)/shard_map/all_to_all | solution.py:17
  98.0 0.0 reduce-scatter.3.cloned.1.call-start
  98.0 0.0 copy-done.3
  98.1 0.2 fusion.2
  98.3 0.1 copy.14
  98.4 8.5 %all-to-all-done = f32[8,64,128]{2,1,0:T(8,128)S(1)} async-done(((f32[8,64,128]{2,1,0:T(8,128)}), f32[8,64,128]{2,1,0:T(8,128)S(1)}, u32[]{:S(2)}, u32[]{:S(2)}) %all-to-all-start) | async-done | bytes 262176 | tf_op jit(solution)/shard_map/all_to_all | solution.py:17
  106.9 0.1 copy.13
  107.0 0.3 fusion.1
  107.3 0.1 copy.15
  107.4 9.3 %all_to_all.10 = bf16[8,64,128]{2,1,0:T(8,128)(2,1)S(1)} all-to-all(bf16[8,64,128]{2,1,0:T(8,128)(2,1)S(1)} %broadcast_in_dim.2), channel_id=1, replica_groups=mesh['atom_0'=2,'atom_1'=8,'atom_2'=2,'band'=8] {'band'}, dimensions={0} | all-to-all | bytes 262144 | tf_op jit(solution)/shard_map/all_to_all | solution.py:23
  116.8 2.3 convolution_bitcast_fusion
  119.1 6.0 %copy.16 = f32[2,16,16,8192]{3,2,1,0:T(8,128)} copy(f32[2,16,16,8192]{3,2,0,1:T(8,128)S(1)} %convolution_bitcast_fusion) | data formatting | bytes 33554432 | tf_op jit(solution)/shard_map/transpose | solution.py:43
  125.2 0.0 reduce-scatter.3.cloned.1.call-update
  125.2 0.0 reduce-scatter.5.cloned.1.call-start
  125.2 27.9 %reduce-scatter.3.cloned.1.call-done = f32[16,16,8192]{2,1,0:T(8,128)} async-done(((f32[32,16,8192]{2,1,0:T(8,128)}), f32[16,16,8192]{2,1,0:T(8,128)}) %reduce-scatter.3.cloned.1.call-update) | async-done | bytes 8388624 | tf_op jit(solution)/shard_map/reduce_scatter | solution.py:44
  153.1 0.0 reduce-scatter.5.cloned.1.call-update
  153.1 104.4 %reduce-scatter.5.cloned.1.call-done = f32[1,16,8192]{2,1,0:T(8,128)} async-done(((f32[16,16,8192]{2,1,0:T(8,128)}), f32[1,16,8192]{2,1,0:T(8,128)}) %reduce-scatter.5.cloned.1.call-update) | async-done | bytes 524304 | tf_op jit(solution)/shard_map/reduce_scatter | solution.py:45
  257.5 1.8 convert_bitcast_fusion
  (8 shorter events, 0.1 us)
Async XLA Ops:
  6.5 78.6 %copy-start = (bf16[128,8192]{1,0:T(8,128)(2,1)S(1)}, bf16[128,8192]{1,0:T(8,128)(2,1)}, u32[]{:S(2)}) copy-start(bf16[128,8192]{1,0:T(8,128)(2,1)} %param.6) | copy-start | bytes 6291460
  6.5 91.5 %copy-start.3 = (s32[16]{0:T(128)S(1)}, s32[16]{0:T(128)}, u32[]{:S(2)}) copy-start(s32[16]{0:T(128)} %param.9) | copy-start | bytes 196
  6.5 91.5 %copy-start.2 = (s32[16]{0:T(128)S(1)}, s32[16]{0:T(128)}, u32[]{:S(2)}) copy-start(s32[16]{0:T(128)} %param.8) | copy-start | bytes 196
  6.5 91.5 %copy-start.1 = (f32[16,8,8]{0,2,1:T(8,128)S(1)}, f32[16,8,8]{0,2,1:T(8,128)}, u32[]{:S(2)}) copy-start(f32[16,8,8]{0,2,1:T(8,128)} %param.7) | copy-start | bytes 12292
  6.5 78.6 %all-gather.2.cloned.1.call-start = ((), (), s32[]{:S(2)}) async-start(), calls=%async_computation.4 | async-start | bytes 8650752 | tf_op jit(solution)/shard_map/all_gather | solution.py:54
  91.5 15.4 %all-to-all-start = ((f32[8,64,128]{2,1,0:T(8,128)}), f32[8,64,128]{2,1,0:T(8,128)S(1)}, u32[]{:S(2)}, u32[]{:S(2)}) async-start(f32[8,64,128]{2,1,0:T(8,128)} %bitcast.4), calls=%async_computation | async-start | bytes 524288 | tf_op jit(solution)/shard_map/all_to_all | solution.py:17
  98.0 55.1 %reduce-scatter.3.cloned.1.call-start = ((), (), s32[]{:S(2)}) async-start(), calls=%async_computation.5 | async-start | bytes 25165824 | tf_op jit(solution)/shard_map/reduce_scatter | solution.py:44
  125.2 132.3 %reduce-scatter.5.cloned.1.call-start = ((), (), s32[]{:S(2)}) async-start(), calls=%async_computation.6 | async-start | bytes 8912896 | tf_op jit(solution)/shard_map/reduce_scatter | solution.py:45
Sparse Core Ops, SparseCore 0:
  9.2 75.8 all-gather.1
  125.3 27.7 reduce-scatter.2
  155.6 101.8 reduce-scatter.4
where the time goes:
time: 266 us
  waiting for transfers between devices  219 us (82%)
  between operations  13.2 us (5%)
  blocking collectives  9.35 us (4%)
  matrix products  9.21 us (3%)
  starting transfers between devices  6.58 us (2%)
  local copies, waits for them, and re-layouts  6.35 us (2%)
    reduce_scatter x1, waiting for transfers between devices, scatter_pairs(): return lax.psum_scatter(blocks, chips, scatter_dimension=0, tiled=True)[0]  104 us
    all_gather x1, waiting for transfers between devices, shards(): lax.all_gather(wave_rows, ATOM, axis=0, tiled=True)  77.8 us
    reduce_scatter x1, waiting for transfers between devices, scatter_pairs(): blocks = lax.psum_scatter(blocks, core, scatter_dimension=0, tiled=True)  27.9 us
    all_to_all x1, blocking collectives, sent_to_all(): lax.all_to_all(jnp.broadcast_to(shard[None], (count, *shard.shape)), axis...  9.35 us
    all_to_all x1, waiting for transfers between devices, sum_at_owner(): lax.all_to_all(cut_along(shard, dim, count), axis, 0, 0, tiled=True)  8.53 us
    all_to_all x1, starting transfers between devices, sum_at_owner(): lax.all_to_all(cut_along(shard, dim, count), axis, 0, 0, tiled=True)  6.47 us
    dot_general x1, matrix products, shards(): lax.dot_general(lax.all_gather(wave_rows, ATOM, axis=0, tiled=True), proj...  6.41 us
    transpose x1, local copies, waits for them, and re-layouts, scatter_pairs(): blocks = blocks.reshape(*sizes, *inside).swapaxes(0, 1).reshape(-1, *inside)  6.05 us
  transfers between devices with their start and end apart: 4, of which 4 were waited for; matrix products, arithmetic and copies ran while one was open for 0% of the time, Pallas kernels for 0%

commit v1 on v0

--- a/solution.py
+++ b/solution.py
@@ -3,6 +3,7 @@
 from jax import lax
 from jax.sharding import Mesh
 from jax.sharding import PartitionSpec as P
+from jax.lax import all_to_all, axis_size
 
 ATOM = ("atom_0", "atom_1", "atom_2")
 
@@ -46,12 +47,19 @@
 
 
 def shards(wave_rows, projectors, dij_table, dij_index, proj_count):
+
+    def _save_joints(q_in, at_axis):
+        value_now = axis_size(ATOM)
+        b_now = jnp.stack([q_in] * value_now, axis=0)
+        reached = all_to_all(b_now, ATOM, 0, 0)
+        return jnp.concatenate(reached, axis=at_axis)
+
     atom_local = dij_index.shape[0]
     kind_total = dij_table.shape[0]
     per_atom = dij_table.shape[1]
     width = atom_local * per_atom
     partial_value = lax.dot_general(
-        lax.all_gather(wave_rows, ATOM, axis=0, tiled=True),
+        _save_joints(wave_rows, 0),
         projectors,
         (((1,), (1,)), ((), ())),
         preferred_element_type=jnp.float32,

time: 266 us -> 381 us (1.43)
  blocking collectives: 9.35 us -> 204 us
  waiting for transfers between devices: 219 us -> 141 us
    all_to_all x0 -> x1, blocking collectives: none -> 195 us  [_save_joints(): reached = all_to_all(b_now, ATOM, 0, 0)]
    all_gather x1 -> x0, waiting for transfers between devices: 77.8 us -> none  [shards(): lax.all_gather(wave_rows, ATOM, axis=0, tiled=True)]
  transfers between devices with their start and end apart: 4 -> 3, of which waited for: 4 -> 3; matrix products, arithmetic and copies ran while one was open for 0% -> 0% of each run, Pallas kernels for 0% -> 0%
where the time goes in v1:
time: 381 us
  blocking collectives  204 us (54%)
  waiting for transfers between devices  141 us (37%)
  between operations  13.5 us (4%)
  local copies, waits for them, and re-layouts  8.45 us (2%)
  starting transfers between devices  6.43 us (2%)
  matrix products  5.84 us (2%)
    all_to_all x1, blocking collectives, _save_joints(): reached = all_to_all(b_now, ATOM, 0, 0)  195 us
    reduce_scatter x1, waiting for transfers between devices, scatter_pairs(): return lax.psum_scatter(blocks, chips, scatter_dimension=0, tiled=True)[0]  104 us
    reduce_scatter x1, waiting for transfers between devices, scatter_pairs(): blocks = lax.psum_scatter(blocks, core, scatter_dimension=0, tiled=True)  29.1 us
    all_to_all x1, blocking collectives, sent_to_all(): lax.all_to_all(jnp.broadcast_to(shard[None], (count, *shard.shape)), axis...  9.42 us
  transfers between devices with their start and end apart: 3, of which 3 were waited for; matrix products, arithmetic and copies ran while one was open for 0% of the time, Pallas kernels for 0%

profile of v1, /device:TPU:1, one launch (start us, length us, event | category | flops | bytes accessed | tf_op | source)
XLA Modules:
  0.0 381.1 jit_solution(9786906605257926729)
XLA Ops:
  6.5 0.0 copy-start
  6.5 2.1 stack.2
  8.6 194.7 %all_to_all.15 = bf16[32,16,8192]{2,1,0:T(8,128)(2,1)S(1)} all-to-all(bf16[32,16,8192]{2,1,0:T(8,128)(2,1)S(1)} %stack.2), channel_id=1, replica_groups=mesh['atom_0'=2,'atom_1'=8,'atom_2'=2,'band'=8] {'atom_0','atom_1','atom..., dimensions={0} | all-to-all | bytes 16777216 | tf_op jit(solution)/shard_map/all_to_all | solution.py:54
  203.4 0.0 copy-done
  203.4 3.0 fusion.1
  206.4 6.4 %all-to-all-start.1 = ((f32[8,64,128]{2,1,0:T(8,128)}), f32[8,64,128]{2,1,0:T(8,128)S(1)}, u32[]{:S(2)}, u32[]{:S(2)}) async-start(f32[8,64,128]{2,1,0:T(8,128)} %fusion.1), calls=%async_computation.1 | async-start | bytes 524288 | tf_op jit(solution)/shard_map/all_to_all | solution.py:18
  212.8 0.0 reduce-scatter.3.cloned.1.call-start
  212.8 0.0 copy-done.3
  212.8 0.0 copy-done.1
  212.9 0.2 fusion.4
  213.1 0.1 copy.14
  213.2 7.3 %all-to-all-done.1 = f32[8,64,128]{2,1,0:T(8,128)S(1)} async-done(((f32[8,64,128]{2,1,0:T(8,128)}), f32[8,64,128]{2,1,0:T(8,128)S(1)}, u32[]{:S(2)}, u32[]{:S(2)}) %all-to-all-start.1) | async-done | bytes 262176 | tf_op jit(solution)/shard_map/all_to_all | solution.py:18
  220.5 0.1 copy.13
  220.6 0.3 fusion.3
  220.9 0.1 copy.15
  221.0 9.4 %all_to_all.16 = bf16[8,64,128]{2,1,0:T(8,128)(2,1)S(1)} all-to-all(bf16[8,64,128]{2,1,0:T(8,128)(2,1)S(1)} %broadcast_in_dim.2), channel_id=1, replica_groups=mesh['atom_0'=2,'atom_1'=8,'atom_2'=2,'band'=8] {'band'}, dimensions={0} | all-to-all | bytes 262144 | tf_op jit(solution)/shard_map/all_to_all | solution.py:24
  230.4 2.3 convolution_bitcast_fusion
  232.7 6.0 %copy.16 = f32[2,16,16,8192]{3,2,1,0:T(8,128)} copy(f32[2,16,16,8192]{3,2,0,1:T(8,128)S(1)} %convolution_bitcast_fusion) | data formatting | bytes 33554432 | tf_op jit(solution)/shard_map/transpose | solution.py:44
  238.8 0.0 reduce-scatter.3.cloned.1.call-update
  238.8 0.0 reduce-scatter.5.cloned.1.call-start
  238.9 29.1 %reduce-scatter.3.cloned.1.call-done = f32[16,16,8192]{2,1,0:T(8,128)} async-done(((f32[32,16,8192]{2,1,0:T(8,128)}), f32[16,16,8192]{2,1,0:T(8,128)}) %reduce-scatter.3.cloned.1.call-update) | async-done | bytes 8388624 | tf_op jit(solution)/shard_map/reduce_scatter | solution.py:45
  268.0 0.0 reduce-scatter.5.cloned.1.call-update
  268.0 104.4 %reduce-scatter.5.cloned.1.call-done = f32[1,16,8192]{2,1,0:T(8,128)} async-done(((f32[16,16,8192]{2,1,0:T(8,128)}), f32[1,16,8192]{2,1,0:T(8,128)}) %reduce-scatter.5.cloned.1.call-update) | async-done | bytes 524304 | tf_op jit(solution)/shard_map/reduce_scatter | solution.py:46
  372.5 1.8 convert_bitcast_fusion
  (7 shorter events, 0.1 us)
Async XLA Ops:
  6.5 196.9 %copy-start = (bf16[128,8192]{1,0:T(8,128)(2,1)S(1)}, bf16[128,8192]{1,0:T(8,128)(2,1)}, u32[]{:S(2)}) copy-start(bf16[128,8192]{1,0:T(8,128)(2,1)} %param.6) | copy-start | bytes 6291460
  203.4 9.4 %copy-start.3 = (s32[16]{0:T(128)S(1)}, s32[16]{0:T(128)}, u32[]{:S(2)}) copy-start(s32[16]{0:T(128)} %param.9) | copy-start | bytes 196
  203.4 9.5 %copy-start.1 = (f32[16,8,8]{0,2,1:T(8,128)S(1)}, f32[16,8,8]{0,2,1:T(8,128)}, u32[]{:S(2)}) copy-start(f32[16,8,8]{0,2,1:T(8,128)} %param.7) | copy-start | bytes 12292
  203.4 9.5 %copy-start.2 = (s32[16]{0:T(128)S(1)}, s32[16]{0:T(128)}, u32[]{:S(2)}) copy-start(s32[16]{0:T(128)} %param.8) | copy-start | bytes 196
  206.4 14.1 %all-to-all-start.1 = ((f32[8,64,128]{2,1,0:T(8,128)}), f32[8,64,128]{2,1,0:T(8,128)S(1)}, u32[]{:S(2)}, u32[]{:S(2)}) async-start(f32[8,64,128]{2,1,0:T(8,128)} %fusion.1), calls=%async_computation.1 | async-start | bytes 524288 | tf_op jit(solution)/shard_map/all_to_all | solution.py:18
  212.8 55.2 %reduce-scatter.3.cloned.1.call-start = ((), (), s32[]{:S(2)}) async-start(), calls=%async_computation.5 | async-start | bytes 25165824 | tf_op jit(solution)/shard_map/reduce_scatter | solution.py:45
  238.8 133.6 %reduce-scatter.5.cloned.1.call-start = ((), (), s32[]{:S(2)}) async-start(), calls=%async_computation.6 | async-start | bytes 8912896 | tf_op jit(solution)/shard_map/reduce_scatter | solution.py:46
Sparse Core Ops, SparseCore 0:
  238.9 29.0 reduce-scatter.2
  270.6 101.8 reduce-scatter.4
